TPU v7x, 32 devices: a whole 2x2x4 slice. The times are simulated.
32 devices in a mesh: ens: 2 (over y), gx: 4 (over x, core), gy: 4 (over z).
Axes of the slice: x: 2, y: 2, z: 4, core: 2. Of those that a mesh axis runs over, the one named last changes fastest.
Arguments:
- log_conductivity: float32 [64, 64, 256], P(('ens', 'gx'), 'gy'), parts along dimension 0, may hold values from -3 to 3
- state: float32 [64, 64, 256], P(('ens', 'gx'), 'gy'), parts along dimension 0, may hold values from -6 to 6
- gradient: float32 [64, 64, 256], P(('ens', 'gx'), 'gy'), parts along dimension 0, may hold values from -60 to 60
- prior_sample: float32 [64, 64, 256], P(('ens', 'gx'), 'gy'), parts along dimension 0, may hold values from -6 to 6
- sensor_cells: int32 [16384], P(('ens', 'gx', 'gy')), parts along dimension 0, may hold values from 0 to 524287, as said below
- noise_precision: float32 [16384], P(('ens', 'gx', 'gy')), parts along dimension 0, may hold values from 20 to 200
Outputs:
- step_field: float32 [64, 64, 256], P(('ens', 'gx'), 'gy'), parts along dimension 0
- residual: float32 [64, 64, 256], P(('ens', 'gx'), 'gy'), parts along dimension 0
There are 2 independent parts, one for each index of `ens`. A program takes and returns all parts, laid end to end along the dimension named above; each array names one. Nothing has to cross between parts.
Inputs may be any that keep to these rules, and one draw needn't show every extreme that they name: `sensor_cells`: sensors t * 512 to (t + 1) * 512 - 1 observe cells inside the block of cells held by the t-th device in the order gx, then gy (blocks of 8 x 16 x 256 cells); a cell may be observed by several sensors.
All inputs are finite; a program needn't handle non-finite values.
Results may differ from a plain program's by a relative error of at most 0.00015.
Values sent between devices are 32-bit elements; how exact they have to be, the bound alone decides.
No kernel may reach another device: no remote copies, remote signals or barrier semaphores. Data moves between devices by JAX's collectives and lax.ppermute only.
A program may use at most 128 MiB of HBM per device.

v0:
```python
import jax
import jax.numpy as jnp
from jax import lax
from jax.sharding import PartitionSpec as P

LEVELS = 3
SWEEPS = 1
COARSE_SWEEPS = 6
CG_ITERS = 2
DAMPING = 0.8
PRIOR_MASS = 0.5
PRIOR_STIFF = 1.0


def extended(x, sides, width):
    for axis, dim in sides:
        peers, length = (lax.axis_size(axis), x.shape[dim])
        up = [(i, (i + 1) % peers) for i in range(peers - 1)]
        down = [(j, i) for i, j in up]
        last = lax.slice_in_dim(x, length - width, length, axis=dim)
        leading = lax.slice_in_dim(x, 0, width, axis=dim)
        before = lax.ppermute(last, axis, up)
        after = lax.ppermute(leading, axis, down)
        x = jnp.concatenate([before, x, after], axis=dim)
    return x


def coarsen_sum(values):
    extent_x, extent_y, extent_z = values.shape
    blocks = values.reshape(extent_x // 2, 2, extent_y // 2, 2, extent_z // 2, 2)
    return blocks.sum(axis=(1, 3, 5))


def refine(values):
    return jnp.repeat(jnp.repeat(jnp.repeat(values, 2, axis=0), 2, axis=1), 2, axis=2)


def neighbours(padded):
    centre = padded[1:-1, 1:-1, :]
    border = jnp.zeros_like(centre[:, :, :1])
    beside = (
        padded[:-2, 1:-1, :],
        padded[2:, 1:-1, :],
        padded[1:-1, :-2, :],
        padded[1:-1, 2:, :],
        jnp.concatenate([border, centre[:, :, :-1]], axis=2),
        jnp.concatenate([centre[:, :, 1:], border], axis=2),
    )
    return (beside, centre)


def summed(entries):
    result = entries[0]
    for entry in entries[1:]:
        result = result + entry
    return result


def inside_flags(index_x, index_y, extent_x, extent_y, extent_z):
    index_z = jnp.arange(extent_z, dtype=jnp.int32)[None, None, :]
    return (
        index_x > 0,
        index_x < extent_x - 1,
        index_y > 0,
        index_y < extent_y - 1,
        index_z > 0,
        index_z < extent_z - 1,
    )


def face_weights(cond_padded, level_scale, interior):
    beside, centre = neighbours(cond_padded)
    return tuple(
        (
            level_scale * jnp.where(is_inner, 0.5 * (centre + neighbour), centre)
            for is_inner, neighbour in zip(interior, beside)
        )
    )


def apply_operator(padded, couplings, diagonal):
    beside, centre = neighbours(padded)
    return diagonal * centre - summed(
        [weight * neighbour for weight, neighbour in zip(couplings, beside)]
    )


def prior_apply(padded):
    beside, centre = neighbours(padded)
    return PRIOR_MASS * centre + PRIOR_STIFF * (6.0 * centre - summed(list(beside)))


def sensitivity(cond_padded, state_padded, probe_padded, interior):
    cond_side, cond_mid = neighbours(cond_padded)
    state_side, state_mid = neighbours(state_padded)
    probe_side, probe_mid = neighbours(probe_padded)
    flux_mid = cond_mid * probe_mid
    return summed(
        [
            jnp.where(is_inner, 0.5 * (flux_mid + cond_near * probe_near), flux_mid)
            * (state_mid - state_near)
            for is_inner, cond_near, probe_near, state_near in zip(
                interior, cond_side, probe_side, state_side
            )
        ]
    )


def misfit_gradient(cond_padded, state_padded, adjoint_padded, interior):
    cond_mid = neighbours(cond_padded)[1]
    state_side, state_mid = neighbours(state_padded)
    adjoint_side, adjoint_mid = neighbours(adjoint_padded)
    return cond_mid * summed(
        [
            jnp.where(is_inner, 0.5, 1.0) * (state_mid - state_near) * (adjoint_mid - adjoint_near)
            for is_inner, state_near, adjoint_near in zip(interior, state_side, adjoint_side)
        ]
    )


def smooth(iterate, source, couplings, diagonal, padder, sweeps):
    for sweep_index in range(sweeps):
        if iterate is None:
            iterate = DAMPING * source / diagonal
        else:
            iterate = (
                iterate
                + DAMPING
                * (source - apply_operator(padder(iterate), couplings, diagonal))
                / diagonal
            )
    return iterate


def vcycle(source, depth_index, operators, padders, coarse_solve):
    if depth_index == len(operators):
        return coarse_solve(source)
    couplings, diagonal = operators[depth_index]
    iterate = smooth(None, source, couplings, diagonal, padders[depth_index], SWEEPS)
    defect = source - apply_operator(padders[depth_index](iterate), couplings, diagonal)
    iterate = iterate + refine(
        vcycle(coarsen_sum(defect), depth_index + 1, operators, padders, coarse_solve)
    )
    return smooth(iterate, source, couplings, diagonal, padders[depth_index], SWEEPS)


def solve(source, operators, padders, coarse_solve):
    iterate = None
    iterate = vcycle(source, 0, operators, padders, coarse_solve)
    return iterate


def plain_pad(values):
    return jnp.pad(values, ((1, 1), (1, 1), (0, 0)))


def assemble(stacked, devices_x):
    pieces, extent_x, extent_y, extent_z = stacked.shape
    arranged = stacked.reshape(devices_x, pieces // devices_x, extent_x, extent_y, extent_z)
    return arranged.transpose(0, 2, 1, 3, 4).reshape(
        devices_x * extent_x, pieces // devices_x * extent_y, extent_z
    )


def norm_sum(residual):
    return lax.psum(jnp.sum(residual * residual), ("gx", "gy"))


def on_device(log_conductivity, state, gradient, prior_sample, sensor_cells, noise_precision):
    devices_x = lax.axis_size("gx")
    devices_y = lax.axis_size("gy")
    place_x = lax.axis_index("gx")
    place_y = lax.axis_index("gy")
    cells_x, cells_y, cells_z = log_conductivity.shape

    def fine_pad(values):
        return extended(values, (("gx", 0), ("gy", 1)), 1)

    def inner_pad(values):
        return extended(values, (("gx", 0), ("gy", 1)), 1)

    def local_flags(depth_index):
        factor = 2**depth_index
        extent_x = cells_x // factor
        extent_y = cells_y // factor
        index_x = place_x * extent_x + jnp.arange(extent_x, dtype=jnp.int32)[:, None, None]
        index_y = place_y * extent_y + jnp.arange(extent_y, dtype=jnp.int32)[None, :, None]
        return inside_flags(
            index_x, index_y, extent_x * devices_x, extent_y * devices_y, cells_z // factor
        )

    cond_levels = [jnp.exp(log_conductivity)]
    for depth_index in range(LEVELS - 1):
        cond_levels.append(coarsen_sum(cond_levels[-1]) / 8.0)
    padders = [fine_pad] + [inner_pad] * (LEVELS - 2)
    operators = []
    cond_padded = None
    for depth_index in range(LEVELS - 1):
        level_padded = padders[depth_index](cond_levels[depth_index])
        if depth_index == 0:
            cond_padded = level_padded
        couplings = face_weights(level_padded, float(2**depth_index), local_flags(depth_index))
        operators.append((couplings, summed(list(couplings))))
    coarsest = LEVELS - 1
    extent_x, extent_y, extent_z = cond_levels[coarsest].shape
    cond_whole = assemble(
        lax.all_gather(cond_levels[coarsest][None], ("gx", "gy"), axis=0, tiled=True), devices_x
    )
    whole_flags = inside_flags(
        jnp.arange(extent_x * devices_x, dtype=jnp.int32)[:, None, None],
        jnp.arange(extent_y * devices_y, dtype=jnp.int32)[None, :, None],
        extent_x * devices_x,
        extent_y * devices_y,
        extent_z,
    )
    coarse_couplings = face_weights(plain_pad(cond_whole), float(2**coarsest), whole_flags)
    coarse_diagonal = summed(list(coarse_couplings))

    def coarse_solve(source):
        gathered = assemble(
            lax.all_gather(source[None], ("gx", "gy"), axis=0, tiled=True), devices_x
        )
        answer = smooth(None, gathered, coarse_couplings, coarse_diagonal, plain_pad, COARSE_SWEEPS)
        return lax.dynamic_slice(
            answer,
            (place_x * extent_x, place_y * extent_y, place_x * 0),
            (extent_x, extent_y, extent_z),
        )

    fine_flags = local_flags(0)
    rows_all = cells_y * devices_y
    sensor_row = sensor_cells // (rows_all * cells_z)
    sensor_column = sensor_cells // cells_z % rows_all
    sensor_depth = sensor_cells % cells_z
    local_cell = (
        (sensor_row - place_x * cells_x) * cells_y + (sensor_column - place_y * cells_y)
    ) * cells_z + sensor_depth
    weight_field = (
        jnp.zeros((cells_x * cells_y * cells_z,), jnp.float32).at[local_cell].add(noise_precision)
    )
    weight_field = weight_field.reshape(cells_x, cells_y, cells_z)
    state_padded = fine_pad(state)
    source = prior_apply(fine_pad(prior_sample)) - gradient
    step_field = jnp.zeros_like(source)
    residual = source
    direction = residual
    norm_now = norm_sum(residual)
    for iteration in range(CG_ITERS):
        direction_padded = fine_pad(direction)
        change = solve(
            sensitivity(cond_padded, state_padded, direction_padded, fine_flags),
            operators,
            padders,
            coarse_solve,
        )
        adjoint = solve(weight_field * change, operators, padders, coarse_solve)
        curved = misfit_gradient(
            cond_padded, state_padded, fine_pad(adjoint), fine_flags
        ) + prior_apply(direction_padded)
        step_length = norm_now / lax.psum(jnp.sum(direction * curved), ("gx", "gy"))
        step_field = step_field + step_length * direction
        residual = residual - step_length * curved
        if iteration + 1 < CG_ITERS:
            norm_next = norm_sum(residual)
            direction = residual + norm_next / norm_now * direction
            norm_now = norm_next
    return (step_field, residual)


def solution(mesh):
    placed = (
        P(("ens", "gx"), "gy", None),
        P(("ens", "gx"), "gy", None),
        P(("ens", "gx"), "gy", None),
        P(("ens", "gx"), "gy", None),
        P(("ens", "gx", "gy")),
        P(("ens", "gx", "gy")),
    )
    return jax.shard_map(
        on_device,
        mesh=mesh,
        in_specs=placed,
        out_specs=(P(("ens", "gx"), "gy", None), P(("ens", "gx"), "gy", None)),
        check_vma=False,
    )
```

profile of v0, /device:TPU:10, one launch (start us, length us, event | category | flops | bytes accessed | tf_op | source)
XLA Modules:
  0.0 712.5 jit_solution(8180663991162468907)
XLA Ops:
  18.4 9.7 %reshape.259 = f32[4,2,8,2,128,2]{5,4,3,2,1,0:T(8,128)} reshape(f32[8,16,256]{2,1,0:T(8,128)S(1)} %exp.3) | data formatting | bytes 262144 | tf_op jit(solution)/shard_map/reshape | solution.py:30
  28.1 4.1 reduce_sum.128
  37.5 30.1 %all-gather.1 = f32[32,4,64]{2,1,0:T(4,128)S(1)} all-gather(f32[2,4,64]{2,1,0:T(4,128)S(1)} %broadcast_multiply_fusion.1), channel_id=3, replica_groups=mesh['ens'=2,'gx'=4,'gy'=4] {'gx','gy'}, dimensions={0}, use_global_device_ids=true | all-gather | bytes 34816 | tf_op jit(solution)/shard_map/all_gather | solution.py:207
  69.7 4.1 collective-permute-start.2
  127.1 9.7 %reshape.258 = f32[4,2,8,2,128,2]{5,4,3,2,1,0:T(8,128)} reshape(f32[8,16,256]{2,1,0:T(8,128)S(1)} %fusion.126) | data formatting | bytes 262144 | tf_op jit(solution)/shard_map/reshape | solution.py:30
  136.9 4.0 reduce_sum.127
  157.7 30.2 %all-gather = f32[32,4,64]{2,1,0:T(4,128)S(1)} all-gather(f32[2,4,64]{2,1,0:T(4,128)S(1)} %reduce_sum.129), channel_id=2, replica_groups=mesh['ens'=2,'gx'=4,'gy'=4] {'gx','gy'}, dimensions={0}, use_global_device_ids=true | all-gather | bytes 34816 | tf_op jit(solution)/shard_map/all_gather | solution.py:221
  234.5 3.9 collective-permute-start.39
  240.9 9.7 %reshape.271 = f32[4,2,8,2,128,2]{5,4,3,2,1,0:T(8,128)} reshape(f32[8,16,256]{2,1,0:T(8,128)S(1)} %fusion.100) | data formatting | bytes 262144 | tf_op jit(solution)/shard_map/reshape | solution.py:30
  250.6 4.0 reduce_sum.131
  263.5 3.9 collective-permute-start.43
  270.3 31.1 %all-gather.2 = f32[32,4,64]{2,1,0:T(4,128)S(1)} all-gather(f32[2,4,64]{2,1,0:T(4,128)S(1)} %reduce_sum.132), channel_id=4, replica_groups=mesh['ens'=2,'gx'=4,'gy'=4] {'gx','gy'}, dimensions={0}, use_global_device_ids=true | all-gather | bytes 34816 | tf_op jit(solution)/shard_map/all_gather | solution.py:221
  344.9 3.9 collective-permute-start.55
  352.5 32.5 %all-reduce.111 = (f32[]{:T(128)}, f32[]{:T(128)}) all-reduce(f32[]{:T(128)} %get-tuple-element.5, f32[]{:T(128)} %get-tuple-element.4), channel_id=1, replica_groups=mesh['ens'=2,'gx'=4,'gy'=4] {'gx','gy'}, use_global_device_ids=true, to_apply=%region_1.0 | all-reduce | flops 2 | bytes 16 | tf_op jit(solution)/shard_map/psum | solution.py:166
  387.0 30.4 %psum.30 = f32[]{:T(128)} all-reduce(f32[]{:T(128)} %multiply_reduce_fusion.1), channel_id=1, replica_groups=mesh['ens'=2,'gx'=4,'gy'=4] {'gx','gy'}, use_global_device_ids=true, to_apply=%region_12.13 | all-reduce | flops 1 | bytes 8 | tf_op jit(solution)/shard_map/psum | solution.py:166
  450.2 9.7 %reshape.281 = f32[4,2,8,2,128,2]{5,4,3,2,1,0:T(8,128)} reshape(f32[8,16,256]{2,1,0:T(8,128)S(1)} %fusion.60) | data formatting | bytes 262144 | tf_op jit(solution)/shard_map/reshape | solution.py:30
  459.9 4.0 reduce_sum.135
  479.5 31.1 %all-gather.3 = f32[32,4,64]{2,1,0:T(4,128)S(1)} all-gather(f32[2,4,64]{2,1,0:T(4,128)S(1)} %reduce_sum.136), channel_id=5, replica_groups=mesh['ens'=2,'gx'=4,'gy'=4] {'gx','gy'}, dimensions={0}, use_global_device_ids=true | all-gather | bytes 34816 | tf_op jit(solution)/shard_map/all_gather | solution.py:221
  554.5 3.9 collective-permute-start.79
  560.9 9.7 %reshape.291 = f32[4,2,8,2,128,2]{5,4,3,2,1,0:T(8,128)} reshape(f32[8,16,256]{2,1,0:T(8,128)S(1)} %fusion.34) | data formatting | bytes 262144 | tf_op jit(solution)/shard_map/reshape | solution.py:30
  570.6 4.0 reduce_sum.137
  592.3 31.5 %all-gather.4 = f32[32,4,64]{2,1,0:T(4,128)S(1)} all-gather(f32[2,4,64]{2,1,0:T(4,128)} %reduce_sum.138), channel_id=6, replica_groups=mesh['ens'=2,'gx'=4,'gy'=4] {'gx','gy'}, dimensions={0}, use_global_device_ids=true | all-gather | bytes 34816 | tf_op jit(solution)/shard_map/all_gather | solution.py:221
  670.5 3.9 collective-permute-start.95
  677.9 32.5 %psum.31 = f32[]{:T(128)} all-reduce(f32[]{:T(128)} %get-tuple-element.8), channel_id=1, replica_groups=mesh['ens'=2,'gx'=4,'gy'=4] {'gx','gy'}, use_global_device_ids=true, to_apply=%region_18.19 | all-reduce | flops 1 | bytes 8 | tf_op jit(solution)/shard_map/psum | solution.py:260
  (570 shorter events, 362.7 us)
Async XLA Ops:
  1.4 66.3 %collective-permute-start = (f32[1,16,256]{2,1,0:T(8,128)S(1)}, f32[1,16,256]{2,1,0:T(8,128)S(1)}, u32[]{:S(2)}, u32[]{:S(2)}) collective-permute-start(f32[1,16,256]{2,1,0:T(8,128)S(1)} %get-tuple-element.130), channel_id=1, source_target_pairs={{0,4},{4,8},{8,12},{1,5},{5,9},{9,13},{2,6},{6,10},{10,14},{3,7},{... | collective-permute-start | bytes 49160 | tf_op jit(solution)/shard_map/ppermute | solution.py:22
  3.3 66.4 %collective-permute-start.1 = (f32[1,16,256]{2,1,0:T(8,128)S(1)}, f32[1,16,256]{2,1,0:T(8,128)S(1)}, u32[]{:S(2)}, u32[]{:S(2)}) collective-permute-start(f32[1,16,256]{2,1,0:T(8,128)S(1)} %get-tuple-element.129), channel_id=1, source_target_pairs={{4,0},{8,4},{12,8},{5,1},{9,5},{13,9},{6,2},{10,6},{14,10},{7,3},{... | collective-permute-start | bytes 49160 | tf_op jit(solution)/shard_map/ppermute | solution.py:23
  7.9 66.0 %collective-permute-start.5 = (f32[1,16,256]{2,1,0:T(8,128)S(1)}, f32[1,16,256]{2,1,0:T(8,128)S(1)}, u32[]{:S(2)}, u32[]{:S(2)}) collective-permute-start(f32[1,16,256]{2,1,0:T(8,128)S(1)} %get-tuple-element.121), channel_id=1, source_target_pairs={{0,4},{4,8},{8,12},{1,5},{5,9},{9,13},{2,6},{6,10},{10,14},{3,7},{... | collective-permute-start | bytes 49160 | tf_op jit(solution)/shard_map/ppermute | solution.py:22
  9.8 67.3 %collective-permute-start.7 = (f32[1,16,256]{2,1,0:T(8,128)S(1)}, f32[1,16,256]{2,1,0:T(8,128)S(1)}, u32[]{:S(2)}, u32[]{:S(2)}) collective-permute-start(f32[1,16,256]{2,1,0:T(8,128)S(1)} %get-tuple-element.122), channel_id=1, source_target_pairs={{4,0},{8,4},{12,8},{5,1},{9,5},{13,9},{6,2},{10,6},{14,10},{7,3},{... | collective-permute-start | bytes 49160 | tf_op jit(solution)/shard_map/ppermute | solution.py:23
  14.2 65.6 %collective-permute-start.4 = (f32[1,16,256]{2,1,0:T(8,128)S(1)}, f32[1,16,256]{2,1,0:T(8,128)S(1)}, u32[]{:S(2)}, u32[]{:S(2)}) collective-permute-start(f32[1,16,256]{2,1,0:T(8,128)S(1)} %get-tuple-element.116), channel_id=1, source_target_pairs={{0,4},{4,8},{8,12},{1,5},{5,9},{9,13},{2,6},{6,10},{10,14},{3,7},{... | collective-permute-start | bytes 49160 | tf_op jit(solution)/shard_map/ppermute | solution.py:22
  67.7 15.3 %collective-permute-start.9 = (f32[1,16,256]{2,1,0:T(8,128)S(1)}, f32[1,16,256]{2,1,0:T(8,128)S(1)}, u32[]{:S(2)}, u32[]{:S(2)}) collective-permute-start(f32[1,16,256]{2,1,0:T(8,128)S(1)} %get-tuple-element.115), channel_id=1, source_target_pairs={{4,0},{8,4},{12,8},{5,1},{9,5},{13,9},{6,2},{10,6},{14,10},{7,3},{... | collective-permute-start | bytes 49160 | tf_op jit(solution)/shard_map/ppermute | solution.py:23
  69.7 13.3 %collective-permute-start.2 = (f32[10,1,256]{2,1,0:T(1,128)S(1)}, f32[10,1,256]{2,1,0:T(1,128)S(1)}, u32[]{:S(2)}, u32[]{:S(2)}) collective-permute-start(f32[10,1,256]{2,1,0:T(1,128)S(1)} %get-tuple-element.67), channel_id=1, source_target_pairs={{0,1},{1,2},{2,3},{4,5},{5,6},{6,7},{8,9},{9,10},{10,11},{12,13},{... | collective-permute-start | bytes 30728 | tf_op jit(solution)/shard_map/ppermute | solution.py:22
  73.9 9.2 %collective-permute-start.3 = (f32[10,1,256]{2,1,0:T(1,128)S(1)}, f32[10,1,256]{2,1,0:T(1,128)S(1)}, u32[]{:S(2)}, u32[]{:S(2)}) collective-permute-start(f32[10,1,256]{2,1,0:T(1,128)S(1)} %get-tuple-element.68), channel_id=1, source_target_pairs={{1,0},{2,1},{3,2},{5,4},{6,5},{7,6},{9,8},{10,9},{11,10},{13,12},{... | collective-permute-start | bytes 30728 | tf_op jit(solution)/shard_map/ppermute | solution.py:23
  77.1 20.3 %collective-permute-start.10 = (f32[10,1,256]{2,1,0:T(1,128)S(1)}, f32[10,1,256]{2,1,0:T(1,128)S(1)}, u32[]{:S(2)}, u32[]{:S(2)}) collective-permute-start(f32[10,1,256]{2,1,0:T(1,128)S(1)} %get-tuple-element.64), channel_id=1, source_target_pairs={{0,1},{1,2},{2,3},{4,5},{5,6},{6,7},{8,9},{9,10},{10,11},{12,13},{... | collective-permute-start | bytes 30728 | tf_op jit(solution)/shard_map/ppermute | solution.py:22
  79.8 20.9 %collective-permute-start.13 = (f32[10,1,256]{2,1,0:T(1,128)S(1)}, f32[10,1,256]{2,1,0:T(1,128)S(1)}, u32[]{:S(2)}, u32[]{:S(2)}) collective-permute-start(f32[10,1,256]{2,1,0:T(1,128)S(1)} %get-tuple-element.63), channel_id=1, source_target_pairs={{1,0},{2,1},{3,2},{5,4},{6,5},{7,6},{9,8},{10,9},{11,10},{13,12},{... | collective-permute-start | bytes 30728 | tf_op jit(solution)/shard_map/ppermute | solution.py:23
  83.2 8.3 %collective-permute-start.6 = (f32[1,16,256]{2,1,0:T(8,128)S(1)}, f32[1,16,256]{2,1,0:T(8,128)S(1)}, u32[]{:S(2)}, u32[]{:S(2)}) collective-permute-start(f32[1,16,256]{2,1,0:T(8,128)S(1)} %get-tuple-element.123), channel_id=1, source_target_pairs={{0,4},{4,8},{8,12},{1,5},{5,9},{9,13},{2,6},{6,10},{10,14},{3,7},{... | collective-permute-start | bytes 49160 | tf_op jit(solution)/shard_map/ppermute | solution.py:22
  85.1 9.6 %collective-permute-start.8 = (f32[1,16,256]{2,1,0:T(8,128)S(1)}, f32[1,16,256]{2,1,0:T(8,128)S(1)}, u32[]{:S(2)}, u32[]{:S(2)}) collective-permute-start(f32[1,16,256]{2,1,0:T(8,128)S(1)} %get-tuple-element.124), channel_id=1, source_target_pairs={{4,0},{8,4},{12,8},{5,1},{9,5},{13,9},{6,2},{10,6},{14,10},{7,3},{... | collective-permute-start | bytes 49160 | tf_op jit(solution)/shard_map/ppermute | solution.py:23
  88.8 13.9 %collective-permute-start.12 = (f32[10,1,256]{2,1,0:T(1,128)S(1)}, f32[10,1,256]{2,1,0:T(1,128)S(1)}, u32[]{:S(2)}, u32[]{:S(2)}) collective-permute-start(f32[10,1,256]{2,1,0:T(1,128)S(1)} %get-tuple-element.61), channel_id=1, source_target_pairs={{0,1},{1,2},{2,3},{4,5},{5,6},{6,7},{8,9},{9,10},{10,11},{12,13},{... | collective-permute-start | bytes 30728 | tf_op jit(solution)/shard_map/ppermute | solution.py:22
  91.5 14.8 %collective-permute-start.15 = (f32[10,1,256]{2,1,0:T(1,128)S(1)}, f32[10,1,256]{2,1,0:T(1,128)S(1)}, u32[]{:S(2)}, u32[]{:S(2)}) collective-permute-start(f32[10,1,256]{2,1,0:T(1,128)S(1)} %get-tuple-element.62), channel_id=1, source_target_pairs={{1,0},{2,1},{3,2},{5,4},{6,5},{7,6},{9,8},{10,9},{11,10},{13,12},{... | collective-permute-start | bytes 30728 | tf_op jit(solution)/shard_map/ppermute | solution.py:23
  94.7 11.6 %collective-permute-start.11 = (f32[10,1,256]{2,1,0:T(1,128)S(1)}, f32[10,1,256]{2,1,0:T(1,128)S(1)}, u32[]{:S(2)}, u32[]{:S(2)}) collective-permute-start(f32[10,1,256]{2,1,0:T(1,128)S(1)} %get-tuple-element.65), channel_id=1, source_target_pairs={{0,1},{1,2},{2,3},{4,5},{5,6},{6,7},{8,9},{9,10},{10,11},{12,13},{... | collective-permute-start | bytes 30728 | tf_op jit(solution)/shard_map/ppermute | solution.py:22
  97.4 8.9 %collective-permute-start.14 = (f32[10,1,256]{2,1,0:T(1,128)S(1)}, f32[10,1,256]{2,1,0:T(1,128)S(1)}, u32[]{:S(2)}, u32[]{:S(2)}) collective-permute-start(f32[10,1,256]{2,1,0:T(1,128)S(1)} %get-tuple-element.66), channel_id=1, source_target_pairs={{1,0},{2,1},{3,2},{5,4},{6,5},{7,6},{9,8},{10,9},{11,10},{13,12},{... | collective-permute-start | bytes 30728 | tf_op jit(solution)/shard_map/ppermute | solution.py:23
  100.7 11.8 %collective-permute-start.20 = (f32[1,8,128]{2,1,0:T(8,128)S(1)}, f32[1,8,128]{2,1,0:T(8,128)S(1)}, u32[]{:S(2)}, u32[]{:S(2)}) collective-permute-start(f32[1,8,128]{2,1,0:T(8,128)S(1)} %get-tuple-element.225), channel_id=1, source_target_pairs={{0,4},{4,8},{8,12},{1,5},{5,9},{9,13},{2,6},{6,10},{10,14},{3,7},{... | collective-permute-start | bytes 12296 | tf_op jit(solution)/shard_map/ppermute | solution.py:22
  102.7 9.9 %collective-permute-start.21 = (f32[1,8,128]{2,1,0:T(8,128)S(1)}, f32[1,8,128]{2,1,0:T(8,128)S(1)}, u32[]{:S(2)}, u32[]{:S(2)}) collective-permute-start(f32[1,8,128]{2,1,0:T(8,128)S(1)} %get-tuple-element.226), channel_id=1, source_target_pairs={{4,0},{8,4},{12,8},{5,1},{9,5},{13,9},{6,2},{10,6},{14,10},{7,3},{... | collective-permute-start | bytes 12296 | tf_op jit(solution)/shard_map/ppermute | solution.py:23
  107.0 11.5 %collective-permute-start.16 = (f32[1,16,256]{2,1,0:T(8,128)S(1)}, f32[1,16,256]{2,1,0:T(8,128)S(1)}, u32[]{:S(2)}, u32[]{:S(2)}) collective-permute-start(f32[1,16,256]{2,1,0:T(8,128)S(1)} %get-tuple-element.113), channel_id=1, source_target_pairs={{0,4},{4,8},{8,12},{1,5},{5,9},{9,13},{2,6},{6,10},{10,14},{3,7},{... | collective-permute-start | bytes 49160 | tf_op jit(solution)/shard_map/ppermute | solution.py:22
  108.9 9.6 %collective-permute-start.17 = (f32[1,16,256]{2,1,0:T(8,128)S(1)}, f32[1,16,256]{2,1,0:T(8,128)S(1)}, u32[]{:S(2)}, u32[]{:S(2)}) collective-permute-start(f32[1,16,256]{2,1,0:T(8,128)S(1)} %get-tuple-element.114), channel_id=1, source_target_pairs={{4,0},{8,4},{12,8},{5,1},{9,5},{13,9},{6,2},{10,6},{14,10},{7,3},{... | collective-permute-start | bytes 49160 | tf_op jit(solution)/shard_map/ppermute | solution.py:23
  112.6 28.4 %collective-permute-start.22 = (f32[6,1,128]{2,1,0:T(1,128)S(1)}, f32[6,1,128]{2,1,0:T(1,128)S(1)}, u32[]{:S(2)}, u32[]{:S(2)}) collective-permute-start(f32[6,1,128]{2,1,0:T(1,128)S(1)} %get-tuple-element.190), channel_id=1, source_target_pairs={{0,1},{1,2},{2,3},{4,5},{5,6},{6,7},{8,9},{9,10},{10,11},{12,13},{... | collective-permute-start | bytes 9224 | tf_op jit(solution)/shard_map/ppermute | solution.py:22
  115.3 25.7 %collective-permute-start.23 = (f32[6,1,128]{2,1,0:T(1,128)S(1)}, f32[6,1,128]{2,1,0:T(1,128)S(1)}, u32[]{:S(2)}, u32[]{:S(2)}) collective-permute-start(f32[6,1,128]{2,1,0:T(1,128)S(1)} %get-tuple-element.189), channel_id=1, source_target_pairs={{1,0},{2,1},{3,2},{5,4},{6,5},{7,6},{9,8},{10,9},{11,10},{13,12},{... | collective-permute-start | bytes 9224 | tf_op jit(solution)/shard_map/ppermute | solution.py:23
  207.1 10.0 %collective-permute-start.32 = (f32[1,16,256]{2,1,0:T(8,128)S(1)}, f32[1,16,256]{2,1,0:T(8,128)S(1)}, u32[]{:S(2)}, u32[]{:S(2)}) collective-permute-start(f32[1,16,256]{2,1,0:T(8,128)S(1)} %get-tuple-element.107), channel_id=1, source_target_pairs={{0,4},{4,8},{8,12},{1,5},{5,9},{9,13},{2,6},{6,10},{10,14},{3,7},{... | collective-permute-start | bytes 49160 | tf_op jit(solution)/shard_map/ppermute | solution.py:22
  209.0 8.1 %collective-permute-start.33 = (f32[1,16,256]{2,1,0:T(8,128)S(1)}, f32[1,16,256]{2,1,0:T(8,128)S(1)}, u32[]{:S(2)}, u32[]{:S(2)}) collective-permute-start(f32[1,16,256]{2,1,0:T(8,128)S(1)} %get-tuple-element.108), channel_id=1, source_target_pairs={{4,0},{8,4},{12,8},{5,1},{9,5},{13,9},{6,2},{10,6},{14,10},{7,3},{... | collective-permute-start | bytes 49160 | tf_op jit(solution)/shard_map/ppermute | solution.py:23
  (139 other events, 3462.5 us)
where the time goes:
time: 717 us; the launch traced here: 712 us
  starting transfers between devices  274 us (38%)
  blocking collectives  250 us (35%)
  local copies, waits for them, and re-layouts  75.6 us (11%)
  other arithmetic  53.2 us (7%)
  waiting for transfers between devices  52.6 us (7%)
  between operations  7.76 us (1%)
    ppermute x48, starting transfers between devices, extended(): after = lax.ppermute(leading, axis, down)  174 us
    all_gather x4, blocking collectives, coarse_solve(): lax.all_gather(source[None], ('gx', 'gy'), axis=0, tiled=True)  124 us
    ppermute x48, starting transfers between devices, extended(): before = lax.ppermute(last, axis, up)  99.9 us
    psum x2, blocking collectives, norm_sum(): return lax.psum(jnp.sum(residual * residual), ('gx', 'gy'))  62.9 us
    reshape x9, local copies, waits for them, and re-layouts, coarsen_sum(): values.reshape(extent_x // 2, 2, extent_y // 2, 2, extent_z // 2, 2)  53.3 us
    ppermute x48, waiting for transfers between devices, extended(): after = lax.ppermute(leading, axis, down)  52.5 us
    psum x1, blocking collectives, on_device(): step_length = norm_now / lax.psum(jnp.sum(direction * curved), ('gx', 'gy'))  32.5 us
    all_gather x1, blocking collectives, on_device(): lax.all_gather(cond_levels[coarsest][None], ('gx', 'gy'), axis=0, tiled=T...  30.1 us
  transfers between devices with their start and end apart: 96, of which 36 were waited for; matrix products, arithmetic and copies ran while one was open for 6% of the time, Pallas kernels for 0%

commit v1 on v0

--- a/solution.py
+++ b/solution.py
@@ -10,6 +10,16 @@
 DAMPING = 0.8
 PRIOR_MASS = 0.5
 PRIOR_STIFF = 1.0
+
+
+def ring_gather(x, axis, dim):
+    ways, here, step = (lax.axis_size(axis), lax.axis_index(axis), x.shape[dim])
+    shape = [n * ways if d == dim else n for d, n in enumerate(x.shape)]
+    full = lax.dynamic_update_slice_in_dim(jnp.zeros(shape, x.dtype), x, here * step, axis=dim)
+    for far in range(1, ways):
+        x = lax.ppermute(x, axis, [(d, (d + 1) % ways) for d in range(ways)])
+        full = lax.dynamic_update_slice_in_dim(full, x, (here - far) % ways * step, axis=dim)
+    return full
 
 
 def extended(x, sides, width):
@@ -217,9 +227,7 @@
     coarse_diagonal = summed(list(coarse_couplings))
 
     def coarse_solve(source):
-        gathered = assemble(
-            lax.all_gather(source[None], ("gx", "gy"), axis=0, tiled=True), devices_x
-        )
+        gathered = assemble(ring_gather(source[None], ("gx", "gy"), 0), devices_x)
         answer = smooth(None, gathered, coarse_couplings, coarse_diagonal, plain_pad, COARSE_SWEEPS)
         return lax.dynamic_slice(
             answer,

time: 717 us -> 934 us (1.30)
  waiting for transfers between devices: 52.6 us -> 375 us
  blocking collectives: 250 us -> 129 us
    ppermute x0 -> x60, waiting for transfers between devices: none -> 319 us  [ring_gather(): x = lax.ppermute(x, axis, [(d, (d + 1) % ways) for d in range(ways)])]
    all_gather x4 -> x0, blocking collectives: 124 us -> none  [coarse_solve(): lax.all_gather(source[None], ('gx', 'gy'), axis=0, tiled=True)]
  transfers between devices with their start and end apart: 96 -> 156, of which waited for: 36 -> 95; matrix products, arithmetic and copies ran while one was open for 6% -> 5% of each run, Pallas kernels for 0% -> 0%
where the time goes in v1:
time: 934 us; the launch traced here: 922 us
  waiting for transfers between devices  375 us (40%)
  starting transfers between devices  283 us (30%)
  blocking collectives  129 us (14%)
  local copies, waits for them, and re-layouts  79.3 us (8%)
  other arithmetic  47.9 us (5%)
    ppermute x60, waiting for transfers between devices, ring_gather(): x = lax.ppermute(x, axis, [(d, (d + 1) % ways) for d in range(ways)])  319 us
    ppermute x48, starting transfers between devices, extended(): after = lax.ppermute(leading, axis, down)  174 us
    ppermute x48, starting transfers between devices, extended(): before = lax.ppermute(last, axis, up)  106 us
    psum x2, blocking collectives, norm_sum(): return lax.psum(jnp.sum(residual * residual), ('gx', 'gy'))  62.9 us
    ppermute x48, waiting for transfers between devices, extended(): after = lax.ppermute(leading, axis, down)  55.3 us
    reshape x9, local copies, waits for them, and re-layouts, coarsen_sum(): values.reshape(extent_x // 2, 2, extent_y // 2, 2, extent_z // 2, 2)  53.3 us
    all_gather x1, blocking collectives, on_device(): lax.all_gather(cond_levels[coarsest][None], ('gx', 'gy'), axis=0, tiled=T...  33.3 us
    psum x1, blocking collectives, on_device(): step_length = norm_now / lax.psum(jnp.sum(direction * curved), ('gx', 'gy'))  32.5 us
  transfers between devices with their start and end apart: 156, of which 95 were waited for; matrix products, arithmetic and copies ran while one was open for 5% of the time, Pallas kernels for 0%

profile of v1, /device:TPU:10, one launch (start us, length us, event | category | flops | bytes accessed | tf_op | source)
XLA Modules:
  0.0 921.7 jit_solution(14611074900826365713)
XLA Ops:
  18.4 9.7 %reshape.259 = f32[4,2,8,2,128,2]{5,4,3,2,1,0:T(8,128)} reshape(f32[8,16,256]{2,1,0:T(8,128)S(1)} %exp.3) | data formatting | bytes 262144 | tf_op jit(solution)/shard_map/reshape | solution.py:40
  92.8 9.7 %reshape.258 = f32[4,2,8,2,128,2]{5,4,3,2,1,0:T(8,128)} reshape(f32[8,16,256]{2,1,0:T(8,128)S(1)} %fusion.126) | data formatting | bytes 262144 | tf_op jit(solution)/shard_map/reshape | solution.py:40
  137.4 33.3 %all-gather = f32[32,4,64]{2,1,0:T(4,128)S(1)} all-gather(f32[2,4,64]{2,1,0:T(4,128)S(1)} %broadcast_multiply_fusion.1), channel_id=2, replica_groups=mesh['ens'=2,'gx'=4,'gy'=4] {'gx','gy'}, dimensions={0}, use_global_device_ids=true | all-gather | bytes 34816 | tf_op jit(solution)/shard_map/all_gather | solution.py:217
  199.5 5.7 collective-permute-done.37
  205.2 5.7 collective-permute-done.38
  211.0 5.7 collective-permute-done.39
  216.7 5.7 collective-permute-done.40
  222.4 5.7 collective-permute-done.41
  288.5 9.7 %reshape.271 = f32[4,2,8,2,128,2]{5,4,3,2,1,0:T(8,128)} reshape(f32[8,16,256]{2,1,0:T(8,128)S(1)} %fusion.100) | data formatting | bytes 262144 | tf_op jit(solution)/shard_map/reshape | solution.py:40
  327.3 5.7 collective-permute-done.61
  333.0 5.7 collective-permute-done.62
  338.7 5.7 collective-permute-done.63
  344.5 5.7 collective-permute-done.64
  350.2 5.7 collective-permute-done.65
  355.9 5.7 collective-permute-done.66
  361.7 5.7 collective-permute-done.67
  367.4 5.7 collective-permute-done.68
  373.1 5.7 collective-permute-done.69
  378.9 5.7 collective-permute-done.70
  454.3 32.5 %all-reduce.111 = (f32[]{:T(128)}, f32[]{:T(128)}) all-reduce(f32[]{:T(128)} %get-tuple-element.5, f32[]{:T(128)} %get-tuple-element.4), channel_id=1, replica_groups=mesh['ens'=2,'gx'=4,'gy'=4] {'gx','gy'}, use_global_device_ids=true, to_apply=%region_1.0 | all-reduce | flops 2 | bytes 16 | tf_op jit(solution)/shard_map/psum | solution.py:176
  488.8 30.4 %psum.30 = f32[]{:T(128)} all-reduce(f32[]{:T(128)} %multiply_reduce_fusion.1), channel_id=1, replica_groups=mesh['ens'=2,'gx'=4,'gy'=4] {'gx','gy'}, use_global_device_ids=true, to_apply=%region_12.13 | all-reduce | flops 1 | bytes 8 | tf_op jit(solution)/shard_map/psum | solution.py:176
  551.9 9.7 %reshape.281 = f32[4,2,8,2,128,2]{5,4,3,2,1,0:T(8,128)} reshape(f32[8,16,256]{2,1,0:T(8,128)S(1)} %fusion.60) | data formatting | bytes 262144 | tf_op jit(solution)/shard_map/reshape | solution.py:40
  716.8 9.7 %reshape.291 = f32[4,2,8,2,128,2]{5,4,3,2,1,0:T(8,128)} reshape(f32[8,16,256]{2,1,0:T(8,128)S(1)} %fusion.34) | data formatting | bytes 262144 | tf_op jit(solution)/shard_map/reshape | solution.py:40
  886.8 32.5 %psum.31 = f32[]{:T(128)} all-reduce(f32[]{:T(128)} %get-tuple-element.8), channel_id=1, replica_groups=mesh['ens'=2,'gx'=4,'gy'=4] {'gx','gy'}, use_global_device_ids=true, to_apply=%region_18.19 | all-reduce | flops 1 | bytes 8 | tf_op jit(solution)/shard_map/psum | solution.py:268
  (714 shorter events, 650.2 us)
Async XLA Ops:
  1.4 31.0 %collective-permute-start = (f32[1,16,256]{2,1,0:T(8,128)S(1)}, f32[1,16,256]{2,1,0:T(8,128)S(1)}, u32[]{:S(2)}, u32[]{:S(2)}) collective-permute-start(f32[1,16,256]{2,1,0:T(8,128)S(1)} %get-tuple-element.130), channel_id=1, source_target_pairs={{0,4},{4,8},{8,12},{1,5},{5,9},{9,13},{2,6},{6,10},{10,14},{3,7},{... | collective-permute-start | bytes 49160 | tf_op jit(solution)/shard_map/ppermute | solution.py:32
  3.3 32.8 %collective-permute-start.1 = (f32[1,16,256]{2,1,0:T(8,128)S(1)}, f32[1,16,256]{2,1,0:T(8,128)S(1)}, u32[]{:S(2)}, u32[]{:S(2)}) collective-permute-start(f32[1,16,256]{2,1,0:T(8,128)S(1)} %get-tuple-element.129), channel_id=1, source_target_pairs={{4,0},{8,4},{12,8},{5,1},{9,5},{13,9},{6,2},{10,6},{14,10},{7,3},{... | collective-permute-start | bytes 49160 | tf_op jit(solution)/shard_map/ppermute | solution.py:33
  7.9 31.7 %collective-permute-start.5 = (f32[1,16,256]{2,1,0:T(8,128)S(1)}, f32[1,16,256]{2,1,0:T(8,128)S(1)}, u32[]{:S(2)}, u32[]{:S(2)}) collective-permute-start(f32[1,16,256]{2,1,0:T(8,128)S(1)} %get-tuple-element.121), channel_id=1, source_target_pairs={{0,4},{4,8},{8,12},{1,5},{5,9},{9,13},{2,6},{6,10},{10,14},{3,7},{... | collective-permute-start | bytes 49160 | tf_op jit(solution)/shard_map/ppermute | solution.py:32
  9.8 32.2 %collective-permute-start.7 = (f32[1,16,256]{2,1,0:T(8,128)S(1)}, f32[1,16,256]{2,1,0:T(8,128)S(1)}, u32[]{:S(2)}, u32[]{:S(2)}) collective-permute-start(f32[1,16,256]{2,1,0:T(8,128)S(1)} %get-tuple-element.122), channel_id=1, source_target_pairs={{4,0},{8,4},{12,8},{5,1},{9,5},{13,9},{6,2},{10,6},{14,10},{7,3},{... | collective-permute-start | bytes 49160 | tf_op jit(solution)/shard_map/ppermute | solution.py:33
  14.2 31.3 %collective-permute-start.4 = (f32[1,16,256]{2,1,0:T(8,128)S(1)}, f32[1,16,256]{2,1,0:T(8,128)S(1)}, u32[]{:S(2)}, u32[]{:S(2)}) collective-permute-start(f32[1,16,256]{2,1,0:T(8,128)S(1)} %get-tuple-element.116), channel_id=1, source_target_pairs={{0,4},{4,8},{8,12},{1,5},{5,9},{9,13},{2,6},{6,10},{10,14},{3,7},{... | collective-permute-start | bytes 49160 | tf_op jit(solution)/shard_map/ppermute | solution.py:32
  32.4 15.6 %collective-permute-start.9 = (f32[1,16,256]{2,1,0:T(8,128)S(1)}, f32[1,16,256]{2,1,0:T(8,128)S(1)}, u32[]{:S(2)}, u32[]{:S(2)}) collective-permute-start(f32[1,16,256]{2,1,0:T(8,128)S(1)} %get-tuple-element.115), channel_id=1, source_target_pairs={{4,0},{8,4},{12,8},{5,1},{9,5},{13,9},{6,2},{10,6},{14,10},{7,3},{... | collective-permute-start | bytes 49160 | tf_op jit(solution)/shard_map/ppermute | solution.py:33
  36.1 11.9 %collective-permute-start.2 = (f32[10,1,256]{2,1,0:T(1,128)S(1)}, f32[10,1,256]{2,1,0:T(1,128)S(1)}, u32[]{:S(2)}, u32[]{:S(2)}) collective-permute-start(f32[10,1,256]{2,1,0:T(1,128)S(1)} %get-tuple-element.67), channel_id=1, source_target_pairs={{0,1},{1,2},{2,3},{4,5},{5,6},{6,7},{8,9},{9,10},{10,11},{12,13},{... | collective-permute-start | bytes 30728 | tf_op jit(solution)/shard_map/ppermute | solution.py:32
  39.6 8.4 collective-permute-start.3
  42.0 21.1 %collective-permute-start.10 = (f32[10,1,256]{2,1,0:T(1,128)S(1)}, f32[10,1,256]{2,1,0:T(1,128)S(1)}, u32[]{:S(2)}, u32[]{:S(2)}) collective-permute-start(f32[10,1,256]{2,1,0:T(1,128)S(1)} %get-tuple-element.64), channel_id=1, source_target_pairs={{0,1},{1,2},{2,3},{4,5},{5,6},{6,7},{8,9},{9,10},{10,11},{12,13},{... | collective-permute-start | bytes 30728 | tf_op jit(solution)/shard_map/ppermute | solution.py:32
  45.5 20.1 %collective-permute-start.13 = (f32[10,1,256]{2,1,0:T(1,128)S(1)}, f32[10,1,256]{2,1,0:T(1,128)S(1)}, u32[]{:S(2)}, u32[]{:S(2)}) collective-permute-start(f32[10,1,256]{2,1,0:T(1,128)S(1)} %get-tuple-element.63), channel_id=1, source_target_pairs={{1,0},{2,1},{3,2},{5,4},{6,5},{7,6},{9,8},{10,9},{11,10},{13,12},{... | collective-permute-start | bytes 30728 | tf_op jit(solution)/shard_map/ppermute | solution.py:33
  48.1 9.1 collective-permute-start.6
  50.1 9.6 %collective-permute-start.8 = (f32[1,16,256]{2,1,0:T(8,128)S(1)}, f32[1,16,256]{2,1,0:T(8,128)S(1)}, u32[]{:S(2)}, u32[]{:S(2)}) collective-permute-start(f32[1,16,256]{2,1,0:T(8,128)S(1)} %get-tuple-element.124), channel_id=1, source_target_pairs={{4,0},{8,4},{12,8},{5,1},{9,5},{13,9},{6,2},{10,6},{14,10},{7,3},{... | collective-permute-start | bytes 49160 | tf_op jit(solution)/shard_map/ppermute | solution.py:33
  53.7 13.9 %collective-permute-start.12 = (f32[10,1,256]{2,1,0:T(1,128)S(1)}, f32[10,1,256]{2,1,0:T(1,128)S(1)}, u32[]{:S(2)}, u32[]{:S(2)}) collective-permute-start(f32[10,1,256]{2,1,0:T(1,128)S(1)} %get-tuple-element.61), channel_id=1, source_target_pairs={{0,1},{1,2},{2,3},{4,5},{5,6},{6,7},{8,9},{9,10},{10,11},{12,13},{... | collective-permute-start | bytes 30728 | tf_op jit(solution)/shard_map/ppermute | solution.py:32
  57.3 14.0 %collective-permute-start.15 = (f32[10,1,256]{2,1,0:T(1,128)S(1)}, f32[10,1,256]{2,1,0:T(1,128)S(1)}, u32[]{:S(2)}, u32[]{:S(2)}) collective-permute-start(f32[10,1,256]{2,1,0:T(1,128)S(1)} %get-tuple-element.62), channel_id=1, source_target_pairs={{1,0},{2,1},{3,2},{5,4},{6,5},{7,6},{9,8},{10,9},{11,10},{13,12},{... | collective-permute-start | bytes 30728 | tf_op jit(solution)/shard_map/ppermute | solution.py:33
  59.7 11.6 %collective-permute-start.11 = (f32[10,1,256]{2,1,0:T(1,128)S(1)}, f32[10,1,256]{2,1,0:T(1,128)S(1)}, u32[]{:S(2)}, u32[]{:S(2)}) collective-permute-start(f32[10,1,256]{2,1,0:T(1,128)S(1)} %get-tuple-element.65), channel_id=1, source_target_pairs={{0,1},{1,2},{2,3},{4,5},{5,6},{6,7},{8,9},{9,10},{10,11},{12,13},{... | collective-permute-start | bytes 30728 | tf_op jit(solution)/shard_map/ppermute | solution.py:32
  63.2 8.1 collective-permute-start.14
  65.7 11.8 %collective-permute-start.20 = (f32[1,8,128]{2,1,0:T(8,128)S(1)}, f32[1,8,128]{2,1,0:T(8,128)S(1)}, u32[]{:S(2)}, u32[]{:S(2)}) collective-permute-start(f32[1,8,128]{2,1,0:T(8,128)S(1)} %get-tuple-element.225), channel_id=1, source_target_pairs={{0,4},{4,8},{8,12},{1,5},{5,9},{9,13},{2,6},{6,10},{10,14},{3,7},{... | collective-permute-start | bytes 12296 | tf_op jit(solution)/shard_map/ppermute | solution.py:32
  67.6 9.9 %collective-permute-start.21 = (f32[1,8,128]{2,1,0:T(8,128)S(1)}, f32[1,8,128]{2,1,0:T(8,128)S(1)}, u32[]{:S(2)}, u32[]{:S(2)}) collective-permute-start(f32[1,8,128]{2,1,0:T(8,128)S(1)} %get-tuple-element.226), channel_id=1, source_target_pairs={{4,0},{8,4},{12,8},{5,1},{9,5},{13,9},{6,2},{10,6},{14,10},{7,3},{... | collective-permute-start | bytes 12296 | tf_op jit(solution)/shard_map/ppermute | solution.py:33
  71.9 11.5 %collective-permute-start.16 = (f32[1,16,256]{2,1,0:T(8,128)S(1)}, f32[1,16,256]{2,1,0:T(8,128)S(1)}, u32[]{:S(2)}, u32[]{:S(2)}) collective-permute-start(f32[1,16,256]{2,1,0:T(8,128)S(1)} %get-tuple-element.113), channel_id=1, source_target_pairs={{0,4},{4,8},{8,12},{1,5},{5,9},{9,13},{2,6},{6,10},{10,14},{3,7},{... | collective-permute-start | bytes 49160 | tf_op jit(solution)/shard_map/ppermute | solution.py:32
  73.8 9.6 %collective-permute-start.17 = (f32[1,16,256]{2,1,0:T(8,128)S(1)}, f32[1,16,256]{2,1,0:T(8,128)S(1)}, u32[]{:S(2)}, u32[]{:S(2)}) collective-permute-start(f32[1,16,256]{2,1,0:T(8,128)S(1)} %get-tuple-element.114), channel_id=1, source_target_pairs={{4,0},{8,4},{12,8},{5,1},{9,5},{13,9},{6,2},{10,6},{14,10},{7,3},{... | collective-permute-start | bytes 49160 | tf_op jit(solution)/shard_map/ppermute | solution.py:33
  77.5 29.1 %collective-permute-start.22 = (f32[6,1,128]{2,1,0:T(1,128)S(1)}, f32[6,1,128]{2,1,0:T(1,128)S(1)}, u32[]{:S(2)}, u32[]{:S(2)}) collective-permute-start(f32[6,1,128]{2,1,0:T(1,128)S(1)} %get-tuple-element.190), channel_id=1, source_target_pairs={{0,1},{1,2},{2,3},{4,5},{5,6},{6,7},{8,9},{9,10},{10,11},{12,13},{... | collective-permute-start | bytes 9224 | tf_op jit(solution)/shard_map/ppermute | solution.py:32
  81.0 25.6 %collective-permute-start.23 = (f32[6,1,128]{2,1,0:T(1,128)S(1)}, f32[6,1,128]{2,1,0:T(1,128)S(1)}, u32[]{:S(2)}, u32[]{:S(2)}) collective-permute-start(f32[6,1,128]{2,1,0:T(1,128)S(1)} %get-tuple-element.189), channel_id=1, source_target_pairs={{1,0},{2,1},{3,2},{5,4},{6,5},{7,6},{9,8},{10,9},{11,10},{13,12},{... | collective-permute-start | bytes 9224 | tf_op jit(solution)/shard_map/ppermute | solution.py:33
  137.4 33.4 %collective-permute-start.31 = (f32[1,2,4,64]{3,0,2,1:T(1,128)S(1)}, f32[1,2,4,64]{3,0,2,1:T(1,128)S(1)}, u32[]{:S(2)}, u32[]{:S(2)}) collective-permute-start(f32[1,2,4,64]{3,0,2,1:T(1,128)S(1)} %collective-permute-done.30), channel_id=1, source_target_pairs={{0,1},{1,2},{2,3},{3,4},{4,5},{5,6},{6,7},{7,8},{8,9},{9,10},{10,1... | collective-permute-start | bytes 6152 | tf_op jit(solution)/shard_map/ppermute | solution.py:20
  254.0 9.8 %collective-permute-start.47 = (f32[1,16,256]{2,1,0:T(8,128)S(1)}, f32[1,16,256]{2,1,0:T(8,128)S(1)}, u32[]{:S(2)}, u32[]{:S(2)}) collective-permute-start(f32[1,16,256]{2,1,0:T(8,128)S(1)} %get-tuple-element.107), channel_id=1, source_target_pairs={{0,4},{4,8},{8,12},{1,5},{5,9},{9,13},{2,6},{6,10},{10,14},{3,7},{... | collective-permute-start | bytes 49160 | tf_op jit(solution)/shard_map/ppermute | solution.py:32
  (181 other events, 3309.3 us)
